TPU v7x, 32 devices: a whole 2x2x4 slice. The times are simulated.
32 devices in a mesh: group: 4 (over z), batch: 8 (over y, x, core).
Axes of the slice: x: 2, y: 2, z: 4, core: 2. Of those that a mesh axis runs over, the one named last changes fastest.
Arguments:
- embeds: bfloat16 [65536, 256], P(('group', 'batch')), may hold values from -6 to 6
- out_grad: bfloat16 [65536, 256], P(('group', 'batch')), may hold values from -48 to 48
- w_query: bfloat16 [256, 256], replicated, may hold values from -0.375 to 0.375
- w_key: bfloat16 [256, 256], replicated, may hold values from -0.375 to 0.375
- w_value: bfloat16 [256, 256], replicated, may hold values from -0.375 to 0.375
- lengths: int32 [128], P(('group', 'batch')), may hold values from 1 to 512, as said below
- item_rows: int32 [65536], P(('group', 'batch')), may hold values from 0 to 2047, as said below
- tile_owner: int32 [512], P(('group', 'batch')), may hold values from 0 to 3, as said below
Outputs:
- table_grad: float32 [8192, 256], P(('group', 'batch'))
Inputs may be any that keep to these rules, and one draw needn't show every extreme that they name: `lengths`: a history's live tokens are its first positions; in every draw some history has exactly 512 live tokens. `tile_owner`: among the first 8 tiles of each device's own tiles, and among the last 8, every group owns exactly 2 tiles. `item_rows`: of the 128 tokens of each tile, at most 32 have rows r with the same r // 256, and in every tile some value of r // 256 is taken by exactly 32 tokens.
All inputs are finite; a program needn't handle non-finite values.
Results may differ from a plain program's by a relative error of at most 0.0024.
The roundings to bfloat16 on the way count: a program that leaves them out, or rounds other values in their place, can miss the bound.
Values may be sent and summed in bfloat16 or wider, within the bound.
No kernel may reach another device: no remote copies, remote signals or barrier semaphores. Data moves between devices by JAX's collectives and lax.ppermute only.
A program may use at most 64 MiB of HBM per device.

v0:
```python
import functools
import math

import jax
import jax.numpy as jnp
from jax import lax
from jax.experimental import pallas as pl
from jax.experimental.pallas import tpu as pltpu
from jax.sharding import PartitionSpec as P


HEADS = 2
ROWS_DEV = 256
EXTRA = 8
BASE = 128
LIMIT = 24 << 20
NT = (((1,), (1,)), ((), ()))
TN = (((0,), (0,)), ((), ()))


def dot(a, b, dims=(((1,), (0,)), ((), ()))):
    return lax.dot_general(a, b, dims, preferred_element_type=jnp.float32)


def digits_row(total, width):
    lane = lax.broadcasted_iota(jnp.int32, (1, width), 1)
    low, mid, high = total % BASE, (total // BASE) % BASE, total // (BASE * BASE)
    row = jnp.where(lane == 0, low, jnp.where(lane == 1, mid, jnp.where(lane == 2, high, 0)))
    return row.astype(jnp.float32)


def total_of_digits(row):
    return row[:, 0:1] + row[:, 1:2] * float(BASE) + row[:, 2:3] * float(BASE * BASE)


def attention_kernel(half, halves, groups, tile, len_h, own_h, *refs):
    first = half == 0
    if first:
        (emb_h, gout_h, wq_h, wk_h, wv_h, rows_h), refs = refs[:6], refs[6:]
        outs, refs = refs[:groups], refs[groups:]
        (wq, wk, wv, emb_next, gout_next, counts), refs = refs[:6], refs[6:]
        (emb, gout, rows), refs = refs[:3], refs[3:]
    else:
        (emb, gout, wq, wk, wv, counts, kept), refs = refs[:7], refs[7:]
        outs, refs = refs[:groups], refs[groups:]
    len_ref, own_ref, q_s, k_s, v_s, dq_s, dk_s, dv_s, tok_s, ext_s, idx_s, sems = refs
    width = emb.shape[1]
    half_seqs = len_ref.shape[0] // halves
    half_tiles = own_ref.shape[0] // halves
    owned = half_tiles // groups
    size = emb.shape[0]
    span = size // half_seqs
    head = width // HEADS
    scale = 1.0 / math.sqrt(head)
    block = span // 2
    sub = block // 2

    def load(source, target, sem):
        return pltpu.make_async_copy(source, target, sem)

    def load_rows(source, target, base, at, count, sem):
        return load(source.at[pl.ds(base + at, count)], target.at[pl.ds(at, count)], sem)

    wait_len, wait_own = load(len_h, len_ref, sems.at[0]), load(own_h, own_ref, sems.at[1])
    if first:
        wait_len.start()
        head_loads = [load(wq_h, wq, sems.at[2]), load(wk_h, wk, sems.at[3])]
        head_loads += [load(wv_h, wv, sems.at[4])]
        wait_rows = load(rows_h, rows, sems.at[5])

        def loads(s):
            low = load_rows(emb_h, emb, 0, s * span, block, sems.at[8 + 3 * s])
            high = load_rows(emb_h, emb, 0, s * span + block, block, sems.at[9 + 3 * s])
            other = load_rows(gout_h, gout, 0, s * span, span, sems.at[10 + 3 * s])
            return low, high, other

        for s in range(half_seqs):
            low, high, other = loads(s)
            low.start()
            if s == 0:
                for c in head_loads:
                    c.start()
            high.start()
            other.start()
        wait_rows.start()
        later = [
            load_rows(emb_h, emb_next, size, 0, size, sems.at[6]),
            load_rows(gout_h, gout_next, size, 0, size, sems.at[7]),
        ]
    wait_own.start()

    def gate(raw, grad, weight):
        grown = jnp.exp2(raw * (-scale * math.log2(math.e)))
        sigma = 1.0 / (1.0 + grown)
        act = raw * scale * sigma
        slope = sigma + act * (1.0 - sigma)
        return (
            (act * weight).astype(jnp.bfloat16),
            (grad * weight * slope).astype(jnp.bfloat16),
        )

    def project(base, at):
        rows_in = emb[pl.ds(base + at, block), :]
        q_s[at:at + block, :] = dot(rows_in, wq[...]).astype(jnp.bfloat16)
        k_s[at:at + block, :] = dot(rows_in, wk[...]).astype(jnp.bfloat16)
        v_s[at:at + block, :] = dot(rows_in, wv[...]).astype(jnp.bfloat16)

    def run(base, count, live):
        if live > block:
            project(base, block)
        lane = lax.broadcasted_iota(jnp.int32, (1, block), 1)
        inverse = 1.0 / jnp.broadcast_to(count, (1, block)).astype(jnp.float32)
        causal = lax.broadcasted_iota(jnp.int32, (sub, sub), 0) <= lax.broadcasted_iota(
            jnp.int32, (sub, sub), 1
        )
        zeros = jnp.zeros((sub, sub), jnp.bfloat16)
        for h in range(HEADS):
            cols = slice(h * head, (h + 1) * head)
            att, sco = {}, {}
            for i in range(live // block):
                weight = jnp.where(lane + i * block < count, inverse, 0.0)
                iq = q_s[i * block:(i + 1) * block, cols]
                ig = gout[pl.ds(base + i * block, block), cols]
                for j in range(i + 1):
                    jk = k_s[j * block:(j + 1) * block, cols]
                    jv = v_s[j * block:(j + 1) * block, cols]
                    raw = dot(jk, iq, NT)
                    grad = dot(jv, ig, NT)
                    if i != j:
                        att[j, i], sco[j, i] = gate(raw, grad, weight)
                        continue
                    low, high = weight[:, :sub], weight[:, sub:]
                    a0, s0 = gate(
                        raw[:sub, :sub], grad[:sub, :sub], jnp.where(causal, low, 0.0)
                    )
                    a1, s1 = gate(raw[:sub, sub:], grad[:sub, sub:], high)
                    a2, s2 = gate(
                        raw[sub:, sub:], grad[sub:, sub:], jnp.where(causal, high, 0.0)
                    )

                    def whole(x, y, z):
                        return jnp.concatenate(
                            [
                                jnp.concatenate([x, y], axis=1),
                                jnp.concatenate([zeros, z], axis=1),
                            ],
                            axis=0,
                        )

                    att[j, i], sco[j, i] = whole(a0, a1, a2), whole(s0, s1, s2)
            for j in range(live // block):
                vg = kg = None
                for i in range(j, live // block):
                    iq = q_s[i * block:(i + 1) * block, cols]
                    ig = gout[pl.ds(base + i * block, block), cols]
                    a, b = dot(att[j, i], ig), dot(sco[j, i], iq)
                    vg = a if vg is None else vg + a
                    kg = b if kg is None else kg + b
                dv_s[j * block:(j + 1) * block, cols] = vg.astype(jnp.bfloat16)
                dk_s[j * block:(j + 1) * block, cols] = (kg * scale).astype(jnp.bfloat16)
            for i in range(live // block):
                qg = None
                for j in range(i + 1):
                    jk = k_s[j * block:(j + 1) * block, cols]
                    c = dot(sco[j, i], jk, TN)
                    qg = c if qg is None else qg + c
                dq_s[i * block:(i + 1) * block, cols] = (qg * scale).astype(jnp.bfloat16)
        token = dot(dq_s[0:live, :], wq[...], NT)
        token = token + dot(dk_s[0:live, :], wk[...], NT)
        token = token + dot(dv_s[0:live, :], wv[...], NT)
        tok_s[pl.ds(base, live), :] = token.astype(jnp.bfloat16)
        if live < span:
            tok_s[pl.ds(base + live, span - live), :] = jnp.zeros((span - live, width), jnp.bfloat16)

    if first:
        for c in head_loads:
            c.wait()
        wait_len.wait()
        for s in range(len_ref.shape[0]):
            counts[s:s + 1, :] = jnp.broadcast_to(len_ref[s], (1, counts.shape[1]))

    def one(s, carry):
        base = pl.multiple_of(s * span, span)
        if first:
            low, high, other = loads(s)
            low.wait()
        project(base, 0)
        if first:
            high.wait()
            other.wait()

            @pl.when(s == half_seqs - 1)
            def _():
                for c in later:
                    c.start()

        if first:
            count = len_ref[half * half_seqs + s]
        else:
            count = jnp.max(counts[pl.ds(half * half_seqs + s, 1), :])
        if first:
            pl.when(count <= block)(functools.partial(run, base, count, block))
            pl.when(count > block)(functools.partial(run, base, count, span))
        else:
            run(base, count, span)
        return carry

    lax.fori_loop(0, half_seqs, one, 0)
    wait_own.wait()

    me = lax.axis_index("group")

    def place(part):
        for g in range(groups):
            idx_s[groups * owned + g] = 0
        for t in range(half_tiles):
            owner = own_ref[part * half_tiles + t]
            seen = idx_s[groups * owned + owner]
            idx_s[owner * owned + seen] = t
            idx_s[groups * owned + owner] = seen + 1

    if first:
        wait_rows.wait()
        total = len_ref[0]
        for s in range(1, len_ref.shape[0]):
            total = total + len_ref[s]
        for k in range(groups):
            ext_s[k] = jnp.zeros(ext_s.shape[1:], jnp.float32)
            ext_s[k, halves * owned:halves * owned + 1, :] = digits_row(total, width)
        for part in range(halves - 1, -1, -1):
            place(part)
            for k in range(groups):
                owner = me ^ k
                for s in range(owned):
                    t = idx_s[owner * owned + s] + part * half_tiles
                    row = rows[pl.ds(t, 1), :]
                    at = part * owned + s
                    ext_s[k, at:at + 1, 0:tile] = (row // ROWS_DEV).astype(jnp.float32)
                    ext_s[k, at:at + 1, tile:2 * tile] = (row % ROWS_DEV).astype(jnp.float32)
        for k in range(groups):
            outs[k][owned * tile:owned * tile + EXTRA, :] = ext_s[k].astype(jnp.bfloat16)
    else:
        place(half)
    for k in range(groups):
        owner = me ^ k
        shift = 0
        if not first and k == groups - 1:
            shift = owned * tile
            outs[k][0:shift, :] = kept[0:shift, :]
            outs[k][2 * shift:2 * shift + EXTRA, :] = kept[shift:shift + EXTRA, :]
        for s in range(owned):
            t = idx_s[owner * owned + s]
            outs[k][shift + s * tile:shift + (s + 1) * tile, :] = tok_s[
                pl.ds(pl.multiple_of(t * tile, tile), tile), :
            ]
    if first:
        for c in later:
            c.wait()


def attention(half, halves, groups, lengths, owners, *given):
    width = given[0].shape[1]
    first = half == 0
    size = given[0].shape[0] // (halves if first else 1)
    seqs, tiles = lengths.shape[0], owners.shape[0]
    span = size * halves // seqs
    tile = size * halves // tiles
    half_seqs, half_tiles = seqs // halves, tiles // halves
    owned = half_tiles // groups
    bf16 = jnp.bfloat16
    box = owned * tile
    flops = half_seqs * (2 * span * width * width * 6 + 10 * span * span * width)
    hbm = pl.BlockSpec(memory_space=pltpu.HBM)
    scratch = []
    if first:
        given = [pltpu.with_memory_space_constraint(a, pltpu.HBM) for a in given]
        specs = [hbm] * len(given)
        shapes = [(box + EXTRA, width)] * groups + [(width, width)] * 3 + [(size, width)] * 2
        shapes = [(s, bf16) for s in shapes] + [((EXTRA, 128), jnp.int32)]
        scratch = [pltpu.VMEM((size, width), bf16)] * 2 + [pltpu.VMEM((tiles, tile), jnp.int32)]
    else:
        specs = vmem(len(given))
        shapes = [(box, width)] * (groups - 1) + [(2 * box + EXTRA, width)]
        shapes = [(s, bf16) for s in shapes]
    small = [pltpu.with_memory_space_constraint(a, pltpu.HBM) for a in (lengths, owners)]
    return list(pl.pallas_call(
        functools.partial(attention_kernel, half, halves, groups, tile),
        in_specs=[hbm, hbm] + specs,
        out_specs=vmem(len(shapes)),
        out_shape=[jax.ShapeDtypeStruct(s, d) for s, d in shapes],
        scratch_shapes=scratch
        + [pltpu.SMEM(lengths.shape, jnp.int32), pltpu.SMEM(owners.shape, jnp.int32)]
        + [pltpu.VMEM((span, width), bf16)] * 6
        + [
            pltpu.VMEM((half_seqs * span, width), bf16),
            pltpu.VMEM((groups, EXTRA, width), jnp.float32),
            pltpu.SMEM((groups * owned + groups,), jnp.int32),
            pltpu.SemaphoreType.DMA((8 + 3 * half_seqs,)),
        ],
        compiler_params=pltpu.CompilerParams(vmem_limit_bytes=LIMIT),
        cost_estimate=pl.CostEstimate(
            flops=flops, bytes_accessed=4 * half_seqs * span * width * 2, transcendentals=0
        ),
    )(*small, *given))


def sums_of(block, boxes, exts, first, owned, tile):
    total = None
    row = lax.broadcasted_iota(jnp.int32, (ROWS_DEV, owned * tile), 0).astype(jnp.float32)
    for box, ext in zip(boxes, exts):
        slots = [ext[first + s:first + s + 1, :].astype(jnp.float32) for s in range(owned)]
        high = jnp.concatenate([r[:, 0:tile] for r in slots], axis=1)
        low = jnp.concatenate([r[:, tile:2 * tile] for r in slots], axis=1)
        key = jnp.where(high == block.astype(jnp.float32), low, -1.0)
        hot = jnp.where(row == key, 1.0, 0.0).astype(jnp.bfloat16)
        part = dot(hot, box[0:owned * tile, :])
        total = part if total is None else total + part
    return total


def live_of(exts, at):
    total = None
    for e in exts:
        row = total_of_digits(e[at:at + 1, :].astype(jnp.float32))
        total = row if total is None else total + row
    return total


def live_rows(total, like):
    width = like.shape[-1]
    row = digits_row(jnp.broadcast_to(total, (1, width)).astype(jnp.int32), width)
    return jnp.broadcast_to(row, (EXTRA, width)).astype(like.dtype)


def exts_of(boxes, base):
    return [b[base:base + EXTRA, :] for b in boxes]


def early_kernel(side, pairs, owned, tile, heads, *refs):
    head, later, out = refs[:heads], refs[heads], refs[-1]
    core = lax.axis_index("batch") % 2
    exts = exts_of(head, owned * tile)
    for p in range(pairs):
        block = 2 * p + (1 - core if side == 0 else core)
        total = sums_of(block, head, exts, 0, owned, tile)
        total = total + sums_of(block, [later], exts[:1], owned, owned, tile)
        out[p * ROWS_DEV:(p + 1) * ROWS_DEV, :] = total.astype(out.dtype)
    if side == 0:
        base = pairs * ROWS_DEV
        out[base:base + EXTRA, :] = live_rows(live_of(exts, 2 * owned), out)
        for n in range(1, heads):
            out[base + n * EXTRA:base + (n + 1) * EXTRA, :] = exts[n]


def near_pair_kernel(pairs, owned, tile, heads, *refs):
    head, refs = refs[:heads], refs[heads:]
    own, got, refs = refs[0], refs[1], refs[2:]
    late, outs = refs[:2 * (heads - 1)], refs[2 * (heads - 1):]
    core, pair = lax.axis_index("batch") % 2, lax.axis_index("batch") // 2
    exts = exts_of(head, owned * tile)
    base = pairs * ROWS_DEV
    live = live_of(exts, 2 * owned) + live_of([got[base:base + 1, :]], 0)
    exts = exts[1:] + [
        got[base + n * EXTRA:base + (n + 1) * EXTRA, :] for n in range(1, heads)
    ]
    for k in range(pairs):
        at = pl.multiple_of((pair ^ k) * ROWS_DEV, ROWS_DEV)
        total = own[pl.ds(at, ROWS_DEV), :] + got[pl.ds(at, ROWS_DEV), :].astype(jnp.float32)
        total = total + sums_of(2 * (pair ^ k) + core, late, exts, owned, owned, tile)
        outs[k][0:ROWS_DEV, :] = total.astype(outs[k].dtype)
        outs[k][ROWS_DEV:ROWS_DEV + EXTRA, :] = live_rows(live, outs[k])


def far_pair_kernel(pairs, slots, tile, *refs):
    boxes, outs = refs[:2], refs[2:]
    core, pair = lax.axis_index("batch") % 2, lax.axis_index("batch") // 2
    exts = exts_of(boxes, slots * tile)
    live = live_of(exts, slots)
    for k in range(pairs):
        block = 2 * (pair ^ k) + core
        total = sums_of(block, boxes, exts, 0, slots, tile)
        outs[k][0:ROWS_DEV, :] = total.astype(outs[k].dtype)
        outs[k][ROWS_DEV:ROWS_DEV + EXTRA, :] = live_rows(live, outs[k])


def gathered(ins):
    total = live = None
    for r in ins:
        part = r[0:ROWS_DEV, :].astype(jnp.float32)
        some = total_of_digits(r[ROWS_DEV:ROWS_DEV + 1, :].astype(jnp.float32))
        total = part if total is None else total + part
        live = some if live is None else live + some
    return total, live


def far_kernel(*refs):
    total, live = gathered(refs[:-1])
    out = refs[-1]
    out[0:ROWS_DEV, :] = total.astype(out.dtype)
    out[ROWS_DEV:ROWS_DEV + EXTRA, :] = live_rows(live, out)


def last_kernel(tokens_all, *refs):
    total, live = gathered(refs[:-1])
    refs[-1][...] = total * (tokens_all / live)


def vmem(n):
    return [pl.BlockSpec(memory_space=pltpu.VMEM)] * n


def call(kernel, shapes, flops, *args):
    return pl.pallas_call(
        kernel,
        in_specs=vmem(len(args)),
        out_specs=vmem(len(shapes)) if isinstance(shapes, list) else vmem(1)[0],
        out_shape=shapes,
        compiler_params=pltpu.CompilerParams(vmem_limit_bytes=LIMIT),
        cost_estimate=pl.CostEstimate(flops=flops, bytes_accessed=1 << 20, transcendentals=0),
    )(*args)


def on_device(groups, batches, embeds, out_grad, w_query, w_key, w_value, lengths, item_rows,
              tile_owner):
    tokens, width = embeds.shape
    halves = 2
    tile = tokens // tile_owner.shape[0]
    owned = tile_owner.shape[0] // halves // groups
    pairs = batches // 2
    rows = item_rows.reshape(-1, tile)
    f32, bf16 = jnp.float32, jnp.bfloat16
    shape = jax.ShapeDtypeStruct
    far = groups - 1
    work = 2 * pairs * ROWS_DEV * width * owned * tile

    def swap(box, k):
        return lax.ppermute(box, "group", [(i, i ^ k) for i in range(groups)])

    def across(box, k):
        return lax.ppermute(box, "batch", [(i, i ^ k) for i in range(batches)])

    near = []
    mine = attention(
        0, halves, groups, lengths, tile_owner, embeds, out_grad, w_query, w_key, w_value, rows
    )
    w_all, (emb_next, gout_next) = mine[groups:groups + 3], mine[groups + 3:groups + 5]
    counts = mine[-1]
    for half in range(halves):
        if half:
            mine = attention(
                half, halves, groups, lengths, tile_owner, emb_next, gout_next, *w_all, counts, mine[far]
            )
        near.append([mine[0]] + [swap(mine[k], k) for k in range(far - 1, 0, -1)])
    away = mine[far]

    def parts_of(kernel, flops, *args):
        return call(
            kernel, [shape((ROWS_DEV + EXTRA, width), f32 if k == 0 else bf16) for k in range(pairs)],
            flops, *args,
        )

    far_parts = parts_of(
        functools.partial(far_pair_kernel, pairs, halves * owned, tile),
        4 * work, away, across(away, 1),
    )
    far_parts = [far_parts[0]] + [across(far_parts[k], 2 * k) for k in range(pairs - 1, 0, -1)]
    tall = pairs * ROWS_DEV
    send, own = [
        call(
            functools.partial(early_kernel, which, pairs, owned, tile, far),
            shape((rows_out, width), kind), (far + 1) * work, *near[0], near[1][0],
        )
        for which, rows_out, kind in ((0, tall + far * EXTRA, bf16), (1, tall, f32))
    ]
    got = across(send, 1)
    late = near[1][1:]
    near_parts = parts_of(
        functools.partial(near_pair_kernel, pairs, owned, tile, far),
        4 * work, *near[0], own, got, *late,
        *[across(box, 1) for box in late],
    )
    near_parts = [near_parts[0]] + [across(near_parts[k], 2 * k) for k in range(pairs - 1, 0, -1)]
    far_sum = call(far_kernel, shape((ROWS_DEV + EXTRA, width), bf16), 1 << 20, *far_parts)
    return call(
        functools.partial(last_kernel, float(tokens * groups * batches)),
        shape((ROWS_DEV, width), f32), 1 << 20, *near_parts, swap(far_sum, far),
    )


def solution(mesh):
    groups, batches = mesh.shape["group"], mesh.shape["batch"]
    both = P(("group", "batch"))
    wide = P(("group", "batch"), None)

    def body(*args):
        return on_device(groups, batches, *args)

    return jax.shard_map(
        body,
        mesh=mesh,
        in_specs=(wide, wide, P(), P(), P(), both, both, both),
        out_specs=wide,
        check_vma=False,
    )
```

profile of v0, /device:TPU:0, one launch (start us, length us, event | category | flops | bytes accessed | tf_op | source)
XLA Modules:
  0.0 45.0 jit_solution(3514215752370907394)
XLA Ops:
  0.0 4.0 %shard_map.82 = (bf16[264,256]{1,0:T(8,128)(2,1)S(1)}, bf16[264,256]{1,0:T(8,128)(2,1)S(1)}, bf16[264,256]{1,0:T(8,128)(2,1)S(1)}, bf16[264,256]{1,0:T(8,128)(2,...) custom-call(s32[4]{0:T(128)} %len_h.3, s32[16]{0:T(128)} %own_h.3, ...), custom_call_target="tpu_custom_call" | custom-call | flops 2147483648 | bytes 2097152 | tf_op jit(solution)/shard_map/pallas_call | solution.py:286
  4.0 4.1 %collective-permute-start = (bf16[264,256]{1,0:T(8,128)(2,1)S(1)}, bf16[264,256]{1,0:T(8,128)(2,1)S(1)}, u32[]{:S(2)}, u32[]{:S(2)}) collective-permute-start(bf16[264,256]{1,0:T(8,128)(2,1)S(1)} %get-tuple-element.28), channel_id=1, source_target_pairs={{0,16},{8,24},{16,0},{24,8},{1,17},{9,25},{17,1},{25,9},{2,18},{10... | collective-permute-start | bytes 405512 | tf_op jit(solution)/shard_map/ppermute | solution.py:437
  8.1 1.6 %collective-permute-start.1 = (bf16[264,256]{1,0:T(8,128)(2,1)S(1)}, bf16[264,256]{1,0:T(8,128)(2,1)S(1)}, u32[]{:S(2)}, u32[]{:S(2)}) collective-permute-start(bf16[264,256]{1,0:T(8,128)(2,1)S(1)} %get-tuple-element.29), channel_id=1, source_target_pairs={{0,8},{8,0},{16,24},{24,16},{1,9},{9,1},{17,25},{25,17},{2,10},{10... | collective-permute-start | bytes 405512 | tf_op jit(solution)/shard_map/ppermute | solution.py:437
  9.7 4.2 %shard_map.83 = (bf16[256,256]{1,0:T(8,128)(2,1)S(1)}, bf16[256,256]{1,0:T(8,128)(2,1)S(1)}, bf16[256,256]{1,0:T(8,128)(2,1)S(1)}, bf16[520,256]{1,0:T(8,128)(2,1)S(1)}) custom-call(s32[4]{0:T(128)} %len_h.3, s32[16]{0:T(128)} %own_h.3, bf16[1024,256]{1,0:T(8,128)(2,1)S(1)} %get-tuple-element.30.refs_0_, bf16[1024,256]{1,0:T(8,128)(2,1)S(1)} %get-tuple-element.31.refs_1_, ...), custom_call_target="tpu_custom_call" | custom-call | flops 2147483648 | bytes 2097152 | tf_op jit(solution)/shard_map/pallas_call | solution.py:286
  13.9 0.1 collective-permute-start.10
  14.0 0.7 %collective-permute-done.refs_1_ = bf16[264,256]{1,0:T(8,128)(2,1)S(1)} collective-permute-done((bf16[264,256]{1,0:T(8,128)(2,1)S(1)}, bf16[264,256]{1,0:T(8,128)(2,1)S(1)}, u32[]{:S(2)}, u32[]{:S(2)}) %collective-permute-start) | collective-permute-done | bytes 135200 | tf_op jit(solution)/shard_map/ppermute | solution.py:437
  14.7 0.2 collective-permute-done.1.refs_2_
  14.9 0.7 %shard_map.85 = bf16[1048,256]{1,0:T(8,128)(2,1)S(1)} custom-call(bf16[264,256]{1,0:T(8,128)(2,1)S(1)} %get-tuple-element.27.refs_0_, bf16[264,256]{1,0:T(8,128)(2,1)S(1)} %collective-permute-done.refs_1_, bf16[264,256]{1,0:T(8,128)(2,1)S(1)} %collective-permute-done.1.refs_2_, bf16[256,256]{1,0:T(8,128)(2,1)S(1)} %get-tuple-element.37.refs_3_), custom_call_target="tpu_custom_call" | custom-call | flops 536870912 | bytes 1048576 | tf_op jit(solution)/shard_map/pallas_call | solution.py:413
  15.6 0.1 collective-permute-start.2
  15.7 1.4 %collective-permute-start.3 = (bf16[256,256]{1,0:T(8,128)(2,1)S(1)}, bf16[256,256]{1,0:T(8,128)(2,1)S(1)}, u32[]{:S(2)}, u32[]{:S(2)}) collective-permute-start(bf16[256,256]{1,0:T(8,128)(2,1)S(1)} %get-tuple-element.38), channel_id=1, source_target_pairs={{0,16},{8,24},{16,0},{24,8},{1,17},{9,25},{17,1},{25,9},{2,18},{10... | collective-permute-start | bytes 393224 | tf_op jit(solution)/shard_map/ppermute | solution.py:437
  17.1 0.0 collective-permute-done.10.refs_1_
  17.1 0.7 %shard_map.87 = (f32[264,256]{1,0:T(8,128)S(1)}, bf16[264,256]{1,0:T(8,128)(2,1)S(1)}, bf16[264,256]{1,0:T(8,128)(2,1)S(1)}, bf16[264,256]{1,0:T(8,128)(2,1)S(1)}) custom-call(bf16[520,256]{1,0:T(8,128)(2,1)S(1)} %get-tuple-element.44.refs_0_, bf16[520,256]{1,0:T(8,128)(2,1)S(1)} %collective-permute-done.10.refs_1_), custom_call_target="tpu_custom_call" | custom-call | flops 536870912 | bytes 1048576 | tf_op jit(solution)/shard_map/pallas_call | solution.py:413
  17.9 4.2 %collective-permute-start.11 = (bf16[264,256]{1,0:T(8,128)(2,1)S(1)}, bf16[264,256]{1,0:T(8,128)(2,1)S(1)}, u32[]{:S(2)}, u32[]{:S(2)}) collective-permute-start(bf16[264,256]{1,0:T(8,128)(2,1)S(1)} %get-tuple-element.46), channel_id=1, source_target_pairs={{0,6},{1,7},{2,4},{3,5},{4,2},{5,3},{6,0},{7,1},{8,14},{9,15},{10,... | collective-permute-start | bytes 405512 | tf_op jit(solution)/shard_map/ppermute | solution.py:440
  22.0 2.4 %collective-permute-start.4 = (bf16[256,256]{1,0:T(8,128)(2,1)S(1)}, bf16[256,256]{1,0:T(8,128)(2,1)S(1)}, u32[]{:S(2)}, u32[]{:S(2)}) collective-permute-start(bf16[256,256]{1,0:T(8,128)(2,1)S(1)} %get-tuple-element.39), channel_id=1, source_target_pairs={{0,8},{8,0},{16,24},{24,16},{1,9},{9,1},{17,25},{25,17},{2,10},{10... | collective-permute-start | bytes 393224 | tf_op jit(solution)/shard_map/ppermute | solution.py:437
  24.5 0.0 collective-permute-start.12
  24.5 0.8 %collective-permute-done.3.refs_5_ = bf16[256,256]{1,0:T(8,128)(2,1)S(1)} collective-permute-done((bf16[256,256]{1,0:T(8,128)(2,1)S(1)}, bf16[256,256]{1,0:T(8,128)(2,1)S(1)}, u32[]{:S(2)}, u32[]{:S(2)}) %collective-permute-start.3) | collective-permute-done | bytes 131104 | tf_op jit(solution)/shard_map/ppermute | solution.py:437
  25.3 2.3 %collective-permute-start.13 = (bf16[264,256]{1,0:T(8,128)(2,1)S(1)}, bf16[264,256]{1,0:T(8,128)(2,1)S(1)}, u32[]{:S(2)}, u32[]{:S(2)}) collective-permute-start(bf16[264,256]{1,0:T(8,128)(2,1)S(1)} %get-tuple-element.48), channel_id=1, source_target_pairs={{0,2},{1,3},{2,0},{3,1},{4,6},{5,7},{6,4},{7,5},{8,10},{9,11},{10,... | collective-permute-start | bytes 405512 | tf_op jit(solution)/shard_map/ppermute | solution.py:440
  27.6 0.5 %collective-permute-done.4.refs_6_ = bf16[256,256]{1,0:T(8,128)(2,1)S(1)} collective-permute-done((bf16[256,256]{1,0:T(8,128)(2,1)S(1)}, bf16[256,256]{1,0:T(8,128)(2,1)S(1)}, u32[]{:S(2)}, u32[]{:S(2)}) %collective-permute-start.4) | collective-permute-done | bytes 131104 | tf_op jit(solution)/shard_map/ppermute | solution.py:437
  28.1 0.0 collective-permute-start.5
  28.1 0.0 collective-permute-done.11.refs_1_
  28.1 0.5 %collective-permute-start.6 = (bf16[256,256]{1,0:T(8,128)(2,1)S(1)}, bf16[256,256]{1,0:T(8,128)(2,1)S(1)}, u32[]{:S(2)}, u32[]{:S(2)}) collective-permute-start(bf16[256,256]{1,0:T(8,128)(2,1)S(1)} %collective-permute-done.4.refs_6_), channel_id=1, source_target_pairs={{0,1},{1,0},{2,3},{3,2},{4,5},{5,4},{6,7},{7,6},{8,9},{9,8},{10,11... | collective-permute-start | bytes 393224 | tf_op jit(solution)/shard_map/ppermute | solution.py:440
  28.6 0.7 %shard_map.84.refs_3_ = f32[1024,256]{1,0:T(8,128)S(1)} custom-call(bf16[264,256]{1,0:T(8,128)(2,1)S(1)} %get-tuple-element.27.refs_0_, bf16[264,256]{1,0:T(8,128)(2,1)S(1)} %collective-permute-done.refs_1_, bf16[264,256]{1,0:T(8,128)(2,1)S(1)} %collective-permute-done.1.refs_2_, bf16[256,256]{1,0:T(8,128)(2,1)S(1)} %get-tuple-element.37.refs_3_), custom_call_target="tpu_custom_call" | custom-call | flops 536870912 | bytes 1048576 | tf_op jit(solution)/shard_map/pallas_call | solution.py:413
  29.3 0.2 collective-permute-done.12.refs_2_
  29.6 1.3 %collective-permute-done.13.refs_3_ = bf16[264,256]{1,0:T(8,128)(2,1)S(1)} collective-permute-done((bf16[264,256]{1,0:T(8,128)(2,1)S(1)}, bf16[264,256]{1,0:T(8,128)(2,1)S(1)}, u32[]{:S(2)}, u32[]{:S(2)}) %collective-permute-start.13) | collective-permute-done | bytes 135200 | tf_op jit(solution)/shard_map/ppermute | solution.py:440
  30.9 0.2 shard_map.88
  31.1 3.7 %collective-permute-start.14 = (bf16[264,256]{1,0:T(8,128)(2,1)S(1)}, bf16[264,256]{1,0:T(8,128)(2,1)S(1)}, u32[]{:S(2)}, u32[]{:S(2)}) collective-permute-start(bf16[264,256]{1,0:T(8,128)(2,1)S(1)} %shard_map.88), channel_id=1, source_target_pairs={{0,24},{8,16},{16,8},{24,0},{1,25},{9,17},{17,9},{25,1},{2,26},{10... | collective-permute-start | bytes 405512 | tf_op jit(solution)/shard_map/ppermute | solution.py:437
  34.9 0.0 collective-permute-done.5.refs_7_
  34.9 0.0 collective-permute-done.6.refs_8_
  34.9 0.0 collective-permute-done.2.refs_4_
  34.9 0.7 %shard_map.86 = (f32[264,256]{1,0:T(8,128)S(1)}, bf16[264,256]{1,0:T(8,128)(2,1)S(1)}, bf16[264,256]{1,0:T(8,128)(2,1)S(1)}, bf16[264,256]{1,0:T(8,128)(2,1)S(1)}) custom-call(bf16[264,256]{1,0:T(8,128)(2,1)S(1)} %get-tuple-element.27.refs_0_, bf16[264,256]{1,0:T(8,128)(2,1)S(1)} %collective-permute-done.refs_1_, ...), custom_call_target="tpu_custom_call" | custom-call | flops 536870912 | bytes 1048576 | tf_op jit(solution)/shard_map/pallas_call | solution.py:413
  35.6 2.8 %collective-permute-start.7 = (bf16[264,256]{1,0:T(8,128)(2,1)S(1)}, bf16[264,256]{1,0:T(8,128)(2,1)S(1)}, u32[]{:S(2)}, u32[]{:S(2)}) collective-permute-start(bf16[264,256]{1,0:T(8,128)(2,1)S(1)} %get-tuple-element.41), channel_id=1, source_target_pairs={{0,6},{1,7},{2,4},{3,5},{4,2},{5,3},{6,0},{7,1},{8,14},{9,15},{10,... | collective-permute-start | bytes 405512 | tf_op jit(solution)/shard_map/ppermute | solution.py:440
  38.4 0.5 %collective-permute-start.8 = (bf16[264,256]{1,0:T(8,128)(2,1)S(1)}, bf16[264,256]{1,0:T(8,128)(2,1)S(1)}, u32[]{:S(2)}, u32[]{:S(2)}) collective-permute-start(bf16[264,256]{1,0:T(8,128)(2,1)S(1)} %get-tuple-element.42), channel_id=1, source_target_pairs={{0,4},{1,5},{2,6},{3,7},{4,0},{5,1},{6,2},{7,3},{8,12},{9,13},{10,... | collective-permute-start | bytes 405512 | tf_op jit(solution)/shard_map/ppermute | solution.py:440
  38.9 0.3 collective-permute-start.9
  39.2 0.0 collective-permute-done.14.refs_4_
  39.2 3.2 %collective-permute-done.7.refs_1_ = bf16[264,256]{1,0:T(8,128)(2,1)S(1)} collective-permute-done((bf16[264,256]{1,0:T(8,128)(2,1)S(1)}, bf16[264,256]{1,0:T(8,128)(2,1)S(1)}, u32[]{:S(2)}, u32[]{:S(2)}) %collective-permute-start.7) | collective-permute-done | bytes 135200 | tf_op jit(solution)/shard_map/ppermute | solution.py:440
  42.4 1.7 %collective-permute-done.8.refs_2_ = bf16[264,256]{1,0:T(8,128)(2,1)S(1)} collective-permute-done((bf16[264,256]{1,0:T(8,128)(2,1)S(1)}, bf16[264,256]{1,0:T(8,128)(2,1)S(1)}, u32[]{:S(2)}, u32[]{:S(2)}) %collective-permute-start.8) | collective-permute-done | bytes 135200 | tf_op jit(solution)/shard_map/ppermute | solution.py:440
  44.1 0.0 collective-permute-done.9.refs_3_
  44.1 0.9 %shard_map.89 = f32[256,256]{1,0:T(8,128)} custom-call(f32[264,256]{1,0:T(8,128)S(1)} %get-tuple-element.40.refs_0_, bf16[264,256]{1,0:T(8,128)(2,1)S(1)} %collective-permute-done.7.refs_1_, bf16[264,256]{1,0:T(8,128)(2,1)S(1)} %collective-permute-done.8.refs_2_, bf16[264,256]{1,0:T(8,128)(2,1)S(1)} %collective-permute-done.9.refs_3_, ...), custom_call_target="tpu_custom_call" | custom-call | flops 1048576 | bytes 1048576 | tf_op jit(solution)/shard_map/pallas_call | solution.py:413
Async XLA Ops:
  4.0 10.7 %collective-permute-start = (bf16[264,256]{1,0:T(8,128)(2,1)S(1)}, bf16[264,256]{1,0:T(8,128)(2,1)S(1)}, u32[]{:S(2)}, u32[]{:S(2)}) collective-permute-start(bf16[264,256]{1,0:T(8,128)(2,1)S(1)} %get-tuple-element.28), channel_id=1, source_target_pairs={{0,16},{8,24},{16,0},{24,8},{1,17},{9,25},{17,1},{25,9},{2,18},{10... | collective-permute-start | bytes 405512 | tf_op jit(solution)/shard_map/ppermute | solution.py:437
  8.1 6.8 %collective-permute-start.1 = (bf16[264,256]{1,0:T(8,128)(2,1)S(1)}, bf16[264,256]{1,0:T(8,128)(2,1)S(1)}, u32[]{:S(2)}, u32[]{:S(2)}) collective-permute-start(bf16[264,256]{1,0:T(8,128)(2,1)S(1)} %get-tuple-element.29), channel_id=1, source_target_pairs={{0,8},{8,0},{16,24},{24,16},{1,9},{9,1},{17,25},{25,17},{2,10},{10... | collective-permute-start | bytes 405512 | tf_op jit(solution)/shard_map/ppermute | solution.py:437
  13.9 3.3 %collective-permute-start.10 = (bf16[520,256]{1,0:T(8,128)(2,1)S(1)}, bf16[520,256]{1,0:T(8,128)(2,1)S(1)}, u32[]{:S(2)}, u32[]{:S(2)}) collective-permute-start(bf16[520,256]{1,0:T(8,128)(2,1)S(1)} %get-tuple-element.44.refs_0_), channel_id=1, source_target_pairs={{0,1},{1,0},{2,3},{3,2},{4,5},{5,4},{6,7},{7,6},{8,9},{9,8},{10,11... | collective-permute-start | bytes 798728 | tf_op jit(solution)/shard_map/ppermute | solution.py:440
  15.6 19.2 %collective-permute-start.2 = (bf16[1048,256]{1,0:T(8,128)(2,1)S(1)}, bf16[1048,256]{1,0:T(8,128)(2,1)S(1)}, u32[]{:S(2)}, u32[]{:S(2)}) collective-permute-start(bf16[1048,256]{1,0:T(8,128)(2,1)S(1)} %shard_map.85), channel_id=1, source_target_pairs={{0,1},{1,0},{2,3},{3,2},{4,5},{5,4},{6,7},{7,6},{8,9},{9,8},{10,11... | collective-permute-start | bytes 1609736 | tf_op jit(solution)/shard_map/ppermute | solution.py:440
  15.7 9.6 %collective-permute-start.3 = (bf16[256,256]{1,0:T(8,128)(2,1)S(1)}, bf16[256,256]{1,0:T(8,128)(2,1)S(1)}, u32[]{:S(2)}, u32[]{:S(2)}) collective-permute-start(bf16[256,256]{1,0:T(8,128)(2,1)S(1)} %get-tuple-element.38), channel_id=1, source_target_pairs={{0,16},{8,24},{16,0},{24,8},{1,17},{9,25},{17,1},{25,9},{2,18},{10... | collective-permute-start | bytes 393224 | tf_op jit(solution)/shard_map/ppermute | solution.py:437
  17.9 10.3 %collective-permute-start.11 = (bf16[264,256]{1,0:T(8,128)(2,1)S(1)}, bf16[264,256]{1,0:T(8,128)(2,1)S(1)}, u32[]{:S(2)}, u32[]{:S(2)}) collective-permute-start(bf16[264,256]{1,0:T(8,128)(2,1)S(1)} %get-tuple-element.46), channel_id=1, source_target_pairs={{0,6},{1,7},{2,4},{3,5},{4,2},{5,3},{6,0},{7,1},{8,14},{9,15},{10,... | collective-permute-start | bytes 405512 | tf_op jit(solution)/shard_map/ppermute | solution.py:440
  22.0 6.1 %collective-permute-start.4 = (bf16[256,256]{1,0:T(8,128)(2,1)S(1)}, bf16[256,256]{1,0:T(8,128)(2,1)S(1)}, u32[]{:S(2)}, u32[]{:S(2)}) collective-permute-start(bf16[256,256]{1,0:T(8,128)(2,1)S(1)} %get-tuple-element.39), channel_id=1, source_target_pairs={{0,8},{8,0},{16,24},{24,16},{1,9},{9,1},{17,25},{25,17},{2,10},{10... | collective-permute-start | bytes 393224 | tf_op jit(solution)/shard_map/ppermute | solution.py:437
  24.5 5.1 %collective-permute-start.12 = (bf16[264,256]{1,0:T(8,128)(2,1)S(1)}, bf16[264,256]{1,0:T(8,128)(2,1)S(1)}, u32[]{:S(2)}, u32[]{:S(2)}) collective-permute-start(bf16[264,256]{1,0:T(8,128)(2,1)S(1)} %get-tuple-element.47), channel_id=1, source_target_pairs={{0,4},{1,5},{2,6},{3,7},{4,0},{5,1},{6,2},{7,3},{8,12},{9,13},{10,... | collective-permute-start | bytes 405512 | tf_op jit(solution)/shard_map/ppermute | solution.py:440
  25.3 5.6 %collective-permute-start.13 = (bf16[264,256]{1,0:T(8,128)(2,1)S(1)}, bf16[264,256]{1,0:T(8,128)(2,1)S(1)}, u32[]{:S(2)}, u32[]{:S(2)}) collective-permute-start(bf16[264,256]{1,0:T(8,128)(2,1)S(1)} %get-tuple-element.48), channel_id=1, source_target_pairs={{0,2},{1,3},{2,0},{3,1},{4,6},{5,7},{6,4},{7,5},{8,10},{9,11},{10,... | collective-permute-start | bytes 405512 | tf_op jit(solution)/shard_map/ppermute | solution.py:440
  28.1 6.7 %collective-permute-start.5 = (bf16[256,256]{1,0:T(8,128)(2,1)S(1)}, bf16[256,256]{1,0:T(8,128)(2,1)S(1)}, u32[]{:S(2)}, u32[]{:S(2)}) collective-permute-start(bf16[256,256]{1,0:T(8,128)(2,1)S(1)} %collective-permute-done.3.refs_5_), channel_id=1, source_target_pairs={{0,1},{1,0},{2,3},{3,2},{4,5},{5,4},{6,7},{7,6},{8,9},{9,8},{10,11... | collective-permute-start | bytes 393224 | tf_op jit(solution)/shard_map/ppermute | solution.py:440
  28.1 6.7 %collective-permute-start.6 = (bf16[256,256]{1,0:T(8,128)(2,1)S(1)}, bf16[256,256]{1,0:T(8,128)(2,1)S(1)}, u32[]{:S(2)}, u32[]{:S(2)}) collective-permute-start(bf16[256,256]{1,0:T(8,128)(2,1)S(1)} %collective-permute-done.4.refs_6_), channel_id=1, source_target_pairs={{0,1},{1,0},{2,3},{3,2},{4,5},{5,4},{6,7},{7,6},{8,9},{9,8},{10,11... | collective-permute-start | bytes 393224 | tf_op jit(solution)/shard_map/ppermute | solution.py:440
  31.1 8.0 %collective-permute-start.14 = (bf16[264,256]{1,0:T(8,128)(2,1)S(1)}, bf16[264,256]{1,0:T(8,128)(2,1)S(1)}, u32[]{:S(2)}, u32[]{:S(2)}) collective-permute-start(bf16[264,256]{1,0:T(8,128)(2,1)S(1)} %shard_map.88), channel_id=1, source_target_pairs={{0,24},{8,16},{16,8},{24,0},{1,25},{9,17},{17,9},{25,1},{2,26},{10... | collective-permute-start | bytes 405512 | tf_op jit(solution)/shard_map/ppermute | solution.py:437
  35.6 6.8 %collective-permute-start.7 = (bf16[264,256]{1,0:T(8,128)(2,1)S(1)}, bf16[264,256]{1,0:T(8,128)(2,1)S(1)}, u32[]{:S(2)}, u32[]{:S(2)}) collective-permute-start(bf16[264,256]{1,0:T(8,128)(2,1)S(1)} %get-tuple-element.41), channel_id=1, source_target_pairs={{0,6},{1,7},{2,4},{3,5},{4,2},{5,3},{6,0},{7,1},{8,14},{9,15},{10,... | collective-permute-start | bytes 405512 | tf_op jit(solution)/shard_map/ppermute | solution.py:440
  38.4 5.7 %collective-permute-start.8 = (bf16[264,256]{1,0:T(8,128)(2,1)S(1)}, bf16[264,256]{1,0:T(8,128)(2,1)S(1)}, u32[]{:S(2)}, u32[]{:S(2)}) collective-permute-start(bf16[264,256]{1,0:T(8,128)(2,1)S(1)} %get-tuple-element.42), channel_id=1, source_target_pairs={{0,4},{1,5},{2,6},{3,7},{4,0},{5,1},{6,2},{7,3},{8,12},{9,13},{10,... | collective-permute-start | bytes 405512 | tf_op jit(solution)/shard_map/ppermute | solution.py:440
  38.9 5.3 %collective-permute-start.9 = (bf16[264,256]{1,0:T(8,128)(2,1)S(1)}, bf16[264,256]{1,0:T(8,128)(2,1)S(1)}, u32[]{:S(2)}, u32[]{:S(2)}) collective-permute-start(bf16[264,256]{1,0:T(8,128)(2,1)S(1)} %get-tuple-element.43), channel_id=1, source_target_pairs={{0,2},{1,3},{2,0},{3,1},{4,6},{5,7},{6,4},{7,5},{8,10},{9,11},{10,... | collective-permute-start | bytes 405512 | tf_op jit(solution)/shard_map/ppermute | solution.py:440
where the time goes:
time: 45.2 us; the launch traced here: 45 us
  starting transfers between devices  24 us (53%)
  Pallas kernels  12.1 us (27%)
  waiting for transfers between devices  8.82 us (20%)
    ppermute x5, starting transfers between devices, swap(): return lax.ppermute(box, 'group', [(i, i ^ k) for i in range(groups)])  13.3 us
    ppermute x10, starting transfers between devices, across(): return lax.ppermute(box, 'batch', [(i, i ^ k) for i in range(batches)])  10.7 us
    pallas_call x2, Pallas kernels, attention(): pl.pallas_call(functools.partial(attention_kernel, half, halves, groups,...  8.16 us
    ppermute x10, waiting for transfers between devices, across(): return lax.ppermute(box, 'batch', [(i, i ^ k) for i in range(batches)])  6.55 us
    pallas_call x6, Pallas kernels, call(): pl.pallas_call(kernel, in_specs=vmem(len(args)), out_specs=vmem(len(shape...  3.95 us
    ppermute x5, waiting for transfers between devices, swap(): return lax.ppermute(box, 'group', [(i, i ^ k) for i in range(groups)])  2.27 us
  transfers between devices with their start and end apart: 15, of which 8 were waited for; matrix products, arithmetic and copies ran while one was open for 0% of the time, Pallas kernels for 16%

commit v1 on v0

--- a/solution.py
+++ b/solution.py
@@ -463,7 +463,10 @@
         functools.partial(far_pair_kernel, pairs, halves * owned, tile),
         4 * work, away, across(away, 1),
     )
-    far_parts = [far_parts[0]] + [across(far_parts[k], 2 * k) for k in range(pairs - 1, 0, -1)]
+    far_parts = [far_parts[0]] + [
+        across(far_parts[k], 2 * k)
+        for k in sorted(range(1, pairs), key=lambda k: (k == pairs // 2, -k))
+    ]
     tall = pairs * ROWS_DEV
     send, own = [
         call(

time: 45.2 us -> 45.2 us (level)
    ppermute x5, starting transfers between devices: 13.3 us -> 12.2 us  [swap(): return lax.ppermute(box, 'group', [(i, i ^ k) for i in range(groups)])]
    ppermute x10, starting transfers between devices: 10.7 us -> 11.5 us  [across(): return lax.ppermute(box, 'batch', [(i, i ^ k) for i in range(batches)])]
    ppermute x10, waiting for transfers between devices: 6.55 us -> 7.26 us  [across(): return lax.ppermute(box, 'batch', [(i, i ^ k) for i in range(batches)])]
    ppermute x5, waiting for transfers between devices: 2.27 us -> 1.78 us  [swap(): return lax.ppermute(box, 'group', [(i, i ^ k) for i in range(groups)])]
  transfers between devices with their start and end apart: 15 -> 15, of which waited for: 8 -> 6; matrix products, arithmetic and copies ran while one was open for 0% -> 0% of each run, Pallas kernels for 16% -> 16%
where the time goes in v1:
time: 45.2 us; the launch traced here: 45 us
  starting transfers between devices  23.8 us (53%)
  Pallas kernels  12.1 us (27%)
  waiting for transfers between devices  9.04 us (20%)
    ppermute x5, starting transfers between devices, swap(): return lax.ppermute(box, 'group', [(i, i ^ k) for i in range(groups)])  12.2 us
    ppermute x10, starting transfers between devices, across(): return lax.ppermute(box, 'batch', [(i, i ^ k) for i in range(batches)])  11.5 us
    pallas_call x2, Pallas kernels, attention(): pl.pallas_call(functools.partial(attention_kernel, half, halves, groups,...  8.16 us
    ppermute x10, waiting for transfers between devices, across(): return lax.ppermute(box, 'batch', [(i, i ^ k) for i in range(batches)])  7.26 us
    pallas_call x6, Pallas kernels, call(): pl.pallas_call(kernel, in_specs=vmem(len(args)), out_specs=vmem(len(shape...  3.95 us
    ppermute x5, waiting for transfers between devices, swap(): return lax.ppermute(box, 'group', [(i, i ^ k) for i in range(groups)])  1.78 us
  transfers between devices with their start and end apart: 15, of which 6 were waited for; matrix products, arithmetic and copies ran while one was open for 0% of the time, Pallas kernels for 16%

profile of v1, /device:TPU:0, one launch (start us, length us, event | category | flops | bytes accessed | tf_op | source)
XLA Modules:
  0.0 45.0 jit_solution(2322516269907596439)
XLA Ops:
  0.0 4.0 %shard_map.82 = (bf16[264,256]{1,0:T(8,128)(2,1)S(1)}, bf16[264,256]{1,0:T(8,128)(2,1)S(1)}, bf16[264,256]{1,0:T(8,128)(2,1)S(1)}, bf16[264,256]{1,0:T(8,128)(2,...) custom-call(s32[4]{0:T(128)} %len_h.3, s32[16]{0:T(128)} %own_h.3, ...), custom_call_target="tpu_custom_call" | custom-call | flops 2147483648 | bytes 2097152 | tf_op jit(solution)/shard_map/pallas_call | solution.py:286
  4.0 4.1 %collective-permute-start = (bf16[264,256]{1,0:T(8,128)(2,1)S(1)}, bf16[264,256]{1,0:T(8,128)(2,1)S(1)}, u32[]{:S(2)}, u32[]{:S(2)}) collective-permute-start(bf16[264,256]{1,0:T(8,128)(2,1)S(1)} %get-tuple-element.28), channel_id=1, source_target_pairs={{0,16},{8,24},{16,0},{24,8},{1,17},{9,25},{17,1},{25,9},{2,18},{10... | collective-permute-start | bytes 405512 | tf_op jit(solution)/shard_map/ppermute | solution.py:437
  8.1 1.6 %collective-permute-start.1 = (bf16[264,256]{1,0:T(8,128)(2,1)S(1)}, bf16[264,256]{1,0:T(8,128)(2,1)S(1)}, u32[]{:S(2)}, u32[]{:S(2)}) collective-permute-start(bf16[264,256]{1,0:T(8,128)(2,1)S(1)} %get-tuple-element.29), channel_id=1, source_target_pairs={{0,8},{8,0},{16,24},{24,16},{1,9},{9,1},{17,25},{25,17},{2,10},{10... | collective-permute-start | bytes 405512 | tf_op jit(solution)/shard_map/ppermute | solution.py:437
  9.7 4.2 %shard_map.83 = (bf16[256,256]{1,0:T(8,128)(2,1)S(1)}, bf16[256,256]{1,0:T(8,128)(2,1)S(1)}, bf16[256,256]{1,0:T(8,128)(2,1)S(1)}, bf16[520,256]{1,0:T(8,128)(2,1)S(1)}) custom-call(s32[4]{0:T(128)} %len_h.3, s32[16]{0:T(128)} %own_h.3, bf16[1024,256]{1,0:T(8,128)(2,1)S(1)} %get-tuple-element.30.refs_0_, bf16[1024,256]{1,0:T(8,128)(2,1)S(1)} %get-tuple-element.31.refs_1_, ...), custom_call_target="tpu_custom_call" | custom-call | flops 2147483648 | bytes 2097152 | tf_op jit(solution)/shard_map/pallas_call | solution.py:286
  13.9 0.1 collective-permute-start.10
  14.0 0.7 %collective-permute-done.refs_1_ = bf16[264,256]{1,0:T(8,128)(2,1)S(1)} collective-permute-done((bf16[264,256]{1,0:T(8,128)(2,1)S(1)}, bf16[264,256]{1,0:T(8,128)(2,1)S(1)}, u32[]{:S(2)}, u32[]{:S(2)}) %collective-permute-start) | collective-permute-done | bytes 135200 | tf_op jit(solution)/shard_map/ppermute | solution.py:437
  14.7 0.2 collective-permute-done.1.refs_2_
  14.9 0.7 %shard_map.85 = bf16[1048,256]{1,0:T(8,128)(2,1)S(1)} custom-call(bf16[264,256]{1,0:T(8,128)(2,1)S(1)} %get-tuple-element.27.refs_0_, bf16[264,256]{1,0:T(8,128)(2,1)S(1)} %collective-permute-done.refs_1_, bf16[264,256]{1,0:T(8,128)(2,1)S(1)} %collective-permute-done.1.refs_2_, bf16[256,256]{1,0:T(8,128)(2,1)S(1)} %get-tuple-element.37.refs_3_), custom_call_target="tpu_custom_call" | custom-call | flops 536870912 | bytes 1048576 | tf_op jit(solution)/shard_map/pallas_call | solution.py:413
  15.6 0.1 collective-permute-start.2
  15.7 1.4 %collective-permute-start.3 = (bf16[256,256]{1,0:T(8,128)(2,1)S(1)}, bf16[256,256]{1,0:T(8,128)(2,1)S(1)}, u32[]{:S(2)}, u32[]{:S(2)}) collective-permute-start(bf16[256,256]{1,0:T(8,128)(2,1)S(1)} %get-tuple-element.38), channel_id=1, source_target_pairs={{0,16},{8,24},{16,0},{24,8},{1,17},{9,25},{17,1},{25,9},{2,18},{10... | collective-permute-start | bytes 393224 | tf_op jit(solution)/shard_map/ppermute | solution.py:437
  17.1 0.0 collective-permute-done.10.refs_1_
  17.1 0.7 %shard_map.87 = (f32[264,256]{1,0:T(8,128)S(1)}, bf16[264,256]{1,0:T(8,128)(2,1)S(1)}, bf16[264,256]{1,0:T(8,128)(2,1)S(1)}, bf16[264,256]{1,0:T(8,128)(2,1)S(1)}) custom-call(bf16[520,256]{1,0:T(8,128)(2,1)S(1)} %get-tuple-element.44.refs_0_, bf16[520,256]{1,0:T(8,128)(2,1)S(1)} %collective-permute-done.10.refs_1_), custom_call_target="tpu_custom_call" | custom-call | flops 536870912 | bytes 1048576 | tf_op jit(solution)/shard_map/pallas_call | solution.py:413
  17.9 4.2 %collective-permute-start.11 = (bf16[264,256]{1,0:T(8,128)(2,1)S(1)}, bf16[264,256]{1,0:T(8,128)(2,1)S(1)}, u32[]{:S(2)}, u32[]{:S(2)}) collective-permute-start(bf16[264,256]{1,0:T(8,128)(2,1)S(1)} %get-tuple-element.46), channel_id=1, source_target_pairs={{0,6},{1,7},{2,4},{3,5},{4,2},{5,3},{6,0},{7,1},{8,14},{9,15},{10,... | collective-permute-start | bytes 405512 | tf_op jit(solution)/shard_map/ppermute | solution.py:440
  22.0 2.4 %collective-permute-start.4 = (bf16[256,256]{1,0:T(8,128)(2,1)S(1)}, bf16[256,256]{1,0:T(8,128)(2,1)S(1)}, u32[]{:S(2)}, u32[]{:S(2)}) collective-permute-start(bf16[256,256]{1,0:T(8,128)(2,1)S(1)} %get-tuple-element.39), channel_id=1, source_target_pairs={{0,8},{8,0},{16,24},{24,16},{1,9},{9,1},{17,25},{25,17},{2,10},{10... | collective-permute-start | bytes 393224 | tf_op jit(solution)/shard_map/ppermute | solution.py:437
  24.5 0.0 collective-permute-start.12
  24.5 0.8 %collective-permute-done.3.refs_5_ = bf16[256,256]{1,0:T(8,128)(2,1)S(1)} collective-permute-done((bf16[256,256]{1,0:T(8,128)(2,1)S(1)}, bf16[256,256]{1,0:T(8,128)(2,1)S(1)}, u32[]{:S(2)}, u32[]{:S(2)}) %collective-permute-start.3) | collective-permute-done | bytes 131104 | tf_op jit(solution)/shard_map/ppermute | solution.py:437
  25.3 3.2 %collective-permute-start.13 = (bf16[264,256]{1,0:T(8,128)(2,1)S(1)}, bf16[264,256]{1,0:T(8,128)(2,1)S(1)}, u32[]{:S(2)}, u32[]{:S(2)}) collective-permute-start(bf16[264,256]{1,0:T(8,128)(2,1)S(1)} %get-tuple-element.48), channel_id=1, source_target_pairs={{0,4},{1,5},{2,6},{3,7},{4,0},{5,1},{6,2},{7,3},{8,12},{9,13},{10,... | collective-permute-start | bytes 405512 | tf_op jit(solution)/shard_map/ppermute | solution.py:440
  28.5 0.0 collective-permute-done.4.refs_6_
  28.5 0.0 collective-permute-start.5
  28.5 0.0 collective-permute-done.11.refs_1_
  28.5 0.5 %collective-permute-start.6 = (bf16[256,256]{1,0:T(8,128)(2,1)S(1)}, bf16[256,256]{1,0:T(8,128)(2,1)S(1)}, u32[]{:S(2)}, u32[]{:S(2)}) collective-permute-start(bf16[256,256]{1,0:T(8,128)(2,1)S(1)} %collective-permute-done.4.refs_6_), channel_id=1, source_target_pairs={{0,1},{1,0},{2,3},{3,2},{4,5},{5,4},{6,7},{7,6},{8,9},{9,8},{10,11... | collective-permute-start | bytes 393224 | tf_op jit(solution)/shard_map/ppermute | solution.py:440
  29.0 0.7 %shard_map.84.refs_3_ = f32[1024,256]{1,0:T(8,128)S(1)} custom-call(bf16[264,256]{1,0:T(8,128)(2,1)S(1)} %get-tuple-element.27.refs_0_, bf16[264,256]{1,0:T(8,128)(2,1)S(1)} %collective-permute-done.refs_1_, bf16[264,256]{1,0:T(8,128)(2,1)S(1)} %collective-permute-done.1.refs_2_, bf16[256,256]{1,0:T(8,128)(2,1)S(1)} %get-tuple-element.37.refs_3_), custom_call_target="tpu_custom_call" | custom-call | flops 536870912 | bytes 1048576 | tf_op jit(solution)/shard_map/pallas_call | solution.py:413
  29.7 0.0 collective-permute-done.12.refs_2_
  29.7 2.3 %collective-permute-done.13.refs_3_ = bf16[264,256]{1,0:T(8,128)(2,1)S(1)} collective-permute-done((bf16[264,256]{1,0:T(8,128)(2,1)S(1)}, bf16[264,256]{1,0:T(8,128)(2,1)S(1)}, u32[]{:S(2)}, u32[]{:S(2)}) %collective-permute-start.13) | collective-permute-done | bytes 135200 | tf_op jit(solution)/shard_map/ppermute | solution.py:440
  32.0 0.2 shard_map.88
  32.2 2.6 %collective-permute-start.14 = (bf16[264,256]{1,0:T(8,128)(2,1)S(1)}, bf16[264,256]{1,0:T(8,128)(2,1)S(1)}, u32[]{:S(2)}, u32[]{:S(2)}) collective-permute-start(bf16[264,256]{1,0:T(8,128)(2,1)S(1)} %shard_map.88), channel_id=1, source_target_pairs={{0,24},{8,16},{16,8},{24,0},{1,25},{9,17},{17,9},{25,1},{2,26},{10... | collective-permute-start | bytes 405512 | tf_op jit(solution)/shard_map/ppermute | solution.py:437
  34.9 0.0 collective-permute-done.5.refs_7_
  34.9 0.0 collective-permute-done.6.refs_8_
  34.9 0.0 collective-permute-done.2.refs_4_
  34.9 0.7 %shard_map.86 = (f32[264,256]{1,0:T(8,128)S(1)}, bf16[264,256]{1,0:T(8,128)(2,1)S(1)}, bf16[264,256]{1,0:T(8,128)(2,1)S(1)}, bf16[264,256]{1,0:T(8,128)(2,1)S(1)}) custom-call(bf16[264,256]{1,0:T(8,128)(2,1)S(1)} %get-tuple-element.27.refs_0_, bf16[264,256]{1,0:T(8,128)(2,1)S(1)} %collective-permute-done.refs_1_, ...), custom_call_target="tpu_custom_call" | custom-call | flops 536870912 | bytes 1048576 | tf_op jit(solution)/shard_map/pallas_call | solution.py:413
  35.6 2.8 %collective-permute-start.7 = (bf16[264,256]{1,0:T(8,128)(2,1)S(1)}, bf16[264,256]{1,0:T(8,128)(2,1)S(1)}, u32[]{:S(2)}, u32[]{:S(2)}) collective-permute-start(bf16[264,256]{1,0:T(8,128)(2,1)S(1)} %get-tuple-element.41), channel_id=1, source_target_pairs={{0,6},{1,7},{2,4},{3,5},{4,2},{5,3},{6,0},{7,1},{8,14},{9,15},{10,... | collective-permute-start | bytes 405512 | tf_op jit(solution)/shard_map/ppermute | solution.py:440
  38.4 0.5 %collective-permute-start.8 = (bf16[264,256]{1,0:T(8,128)(2,1)S(1)}, bf16[264,256]{1,0:T(8,128)(2,1)S(1)}, u32[]{:S(2)}, u32[]{:S(2)}) collective-permute-start(bf16[264,256]{1,0:T(8,128)(2,1)S(1)} %get-tuple-element.42), channel_id=1, source_target_pairs={{0,4},{1,5},{2,6},{3,7},{4,0},{5,1},{6,2},{7,3},{8,12},{9,13},{10,... | collective-permute-start | bytes 405512 | tf_op jit(solution)/shard_map/ppermute | solution.py:440
  38.9 0.3 collective-permute-start.9
  39.2 0.0 collective-permute-done.14.refs_4_
  39.2 3.2 %collective-permute-done.7.refs_1_ = bf16[264,256]{1,0:T(8,128)(2,1)S(1)} collective-permute-done((bf16[264,256]{1,0:T(8,128)(2,1)S(1)}, bf16[264,256]{1,0:T(8,128)(2,1)S(1)}, u32[]{:S(2)}, u32[]{:S(2)}) %collective-permute-start.7) | collective-permute-done | bytes 135200 | tf_op jit(solution)/shard_map/ppermute | solution.py:440
  42.4 1.7 %collective-permute-done.8.refs_2_ = bf16[264,256]{1,0:T(8,128)(2,1)S(1)} collective-permute-done((bf16[264,256]{1,0:T(8,128)(2,1)S(1)}, bf16[264,256]{1,0:T(8,128)(2,1)S(1)}, u32[]{:S(2)}, u32[]{:S(2)}) %collective-permute-start.8) | collective-permute-done | bytes 135200 | tf_op jit(solution)/shard_map/ppermute | solution.py:440
  44.1 0.0 collective-permute-done.9.refs_3_
  44.1 0.9 %shard_map.89 = f32[256,256]{1,0:T(8,128)} custom-call(f32[264,256]{1,0:T(8,128)S(1)} %get-tuple-element.40.refs_0_, bf16[264,256]{1,0:T(8,128)(2,1)S(1)} %collective-permute-done.7.refs_1_, bf16[264,256]{1,0:T(8,128)(2,1)S(1)} %collective-permute-done.8.refs_2_, bf16[264,256]{1,0:T(8,128)(2,1)S(1)} %collective-permute-done.9.refs_3_, ...), custom_call_target="tpu_custom_call" | custom-call | flops 1048576 | bytes 1048576 | tf_op jit(solution)/shard_map/pallas_call | solution.py:413
Async XLA Ops:
  4.0 10.7 %collective-permute-start = (bf16[264,256]{1,0:T(8,128)(2,1)S(1)}, bf16[264,256]{1,0:T(8,128)(2,1)S(1)}, u32[]{:S(2)}, u32[]{:S(2)}) collective-permute-start(bf16[264,256]{1,0:T(8,128)(2,1)S(1)} %get-tuple-element.28), channel_id=1, source_target_pairs={{0,16},{8,24},{16,0},{24,8},{1,17},{9,25},{17,1},{25,9},{2,18},{10... | collective-permute-start | bytes 405512 | tf_op jit(solution)/shard_map/ppermute | solution.py:437
  8.1 6.8 %collective-permute-start.1 = (bf16[264,256]{1,0:T(8,128)(2,1)S(1)}, bf16[264,256]{1,0:T(8,128)(2,1)S(1)}, u32[]{:S(2)}, u32[]{:S(2)}) collective-permute-start(bf16[264,256]{1,0:T(8,128)(2,1)S(1)} %get-tuple-element.29), channel_id=1, source_target_pairs={{0,8},{8,0},{16,24},{24,16},{1,9},{9,1},{17,25},{25,17},{2,10},{10... | collective-permute-start | bytes 405512 | tf_op jit(solution)/shard_map/ppermute | solution.py:437
  13.9 3.3 %collective-permute-start.10 = (bf16[520,256]{1,0:T(8,128)(2,1)S(1)}, bf16[520,256]{1,0:T(8,128)(2,1)S(1)}, u32[]{:S(2)}, u32[]{:S(2)}) collective-permute-start(bf16[520,256]{1,0:T(8,128)(2,1)S(1)} %get-tuple-element.44.refs_0_), channel_id=1, source_target_pairs={{0,1},{1,0},{2,3},{3,2},{4,5},{5,4},{6,7},{7,6},{8,9},{9,8},{10,11... | collective-permute-start | bytes 798728 | tf_op jit(solution)/shard_map/ppermute | solution.py:440
  15.6 19.3 %collective-permute-start.2 = (bf16[1048,256]{1,0:T(8,128)(2,1)S(1)}, bf16[1048,256]{1,0:T(8,128)(2,1)S(1)}, u32[]{:S(2)}, u32[]{:S(2)}) collective-permute-start(bf16[1048,256]{1,0:T(8,128)(2,1)S(1)} %shard_map.85), channel_id=1, source_target_pairs={{0,1},{1,0},{2,3},{3,2},{4,5},{5,4},{6,7},{7,6},{8,9},{9,8},{10,11... | collective-permute-start | bytes 1609736 | tf_op jit(solution)/shard_map/ppermute | solution.py:440
  15.7 9.6 %collective-permute-start.3 = (bf16[256,256]{1,0:T(8,128)(2,1)S(1)}, bf16[256,256]{1,0:T(8,128)(2,1)S(1)}, u32[]{:S(2)}, u32[]{:S(2)}) collective-permute-start(bf16[256,256]{1,0:T(8,128)(2,1)S(1)} %get-tuple-element.38), channel_id=1, source_target_pairs={{0,16},{8,24},{16,0},{24,8},{1,17},{9,25},{17,1},{25,9},{2,18},{10... | collective-permute-start | bytes 393224 | tf_op jit(solution)/shard_map/ppermute | solution.py:437
  17.9 10.6 %collective-permute-start.11 = (bf16[264,256]{1,0:T(8,128)(2,1)S(1)}, bf16[264,256]{1,0:T(8,128)(2,1)S(1)}, u32[]{:S(2)}, u32[]{:S(2)}) collective-permute-start(bf16[264,256]{1,0:T(8,128)(2,1)S(1)} %get-tuple-element.46), channel_id=1, source_target_pairs={{0,6},{1,7},{2,4},{3,5},{4,2},{5,3},{6,0},{7,1},{8,14},{9,15},{10,... | collective-permute-start | bytes 405512 | tf_op jit(solution)/shard_map/ppermute | solution.py:440
  22.0 6.4 %collective-permute-start.4 = (bf16[256,256]{1,0:T(8,128)(2,1)S(1)}, bf16[256,256]{1,0:T(8,128)(2,1)S(1)}, u32[]{:S(2)}, u32[]{:S(2)}) collective-permute-start(bf16[256,256]{1,0:T(8,128)(2,1)S(1)} %get-tuple-element.39), channel_id=1, source_target_pairs={{0,8},{8,0},{16,24},{24,16},{1,9},{9,1},{17,25},{25,17},{2,10},{10... | collective-permute-start | bytes 393224 | tf_op jit(solution)/shard_map/ppermute | solution.py:437
  24.5 5.2 %collective-permute-start.12 = (bf16[264,256]{1,0:T(8,128)(2,1)S(1)}, bf16[264,256]{1,0:T(8,128)(2,1)S(1)}, u32[]{:S(2)}, u32[]{:S(2)}) collective-permute-start(bf16[264,256]{1,0:T(8,128)(2,1)S(1)} %get-tuple-element.47), channel_id=1, source_target_pairs={{0,2},{1,3},{2,0},{3,1},{4,6},{5,7},{6,4},{7,5},{8,10},{9,11},{10,... | collective-permute-start | bytes 405512 | tf_op jit(solution)/shard_map/ppermute | solution.py:440
  25.3 6.7 %collective-permute-start.13 = (bf16[264,256]{1,0:T(8,128)(2,1)S(1)}, bf16[264,256]{1,0:T(8,128)(2,1)S(1)}, u32[]{:S(2)}, u32[]{:S(2)}) collective-permute-start(bf16[264,256]{1,0:T(8,128)(2,1)S(1)} %get-tuple-element.48), channel_id=1, source_target_pairs={{0,4},{1,5},{2,6},{3,7},{4,0},{5,1},{6,2},{7,3},{8,12},{9,13},{10,... | collective-permute-start | bytes 405512 | tf_op jit(solution)/shard_map/ppermute | solution.py:440
  28.5 6.4 %collective-permute-start.5 = (bf16[256,256]{1,0:T(8,128)(2,1)S(1)}, bf16[256,256]{1,0:T(8,128)(2,1)S(1)}, u32[]{:S(2)}, u32[]{:S(2)}) collective-permute-start(bf16[256,256]{1,0:T(8,128)(2,1)S(1)} %collective-permute-done.3.refs_5_), channel_id=1, source_target_pairs={{0,1},{1,0},{2,3},{3,2},{4,5},{5,4},{6,7},{7,6},{8,9},{9,8},{10,11... | collective-permute-start | bytes 393224 | tf_op jit(solution)/shard_map/ppermute | solution.py:440
  28.5 6.4 %collective-permute-start.6 = (bf16[256,256]{1,0:T(8,128)(2,1)S(1)}, bf16[256,256]{1,0:T(8,128)(2,1)S(1)}, u32[]{:S(2)}, u32[]{:S(2)}) collective-permute-start(bf16[256,256]{1,0:T(8,128)(2,1)S(1)} %collective-permute-done.4.refs_6_), channel_id=1, source_target_pairs={{0,1},{1,0},{2,3},{3,2},{4,5},{5,4},{6,7},{7,6},{8,9},{9,8},{10,11... | collective-permute-start | bytes 393224 | tf_op jit(solution)/shard_map/ppermute | solution.py:440
  32.2 6.9 %collective-permute-start.14 = (bf16[264,256]{1,0:T(8,128)(2,1)S(1)}, bf16[264,256]{1,0:T(8,128)(2,1)S(1)}, u32[]{:S(2)}, u32[]{:S(2)}) collective-permute-start(bf16[264,256]{1,0:T(8,128)(2,1)S(1)} %shard_map.88), channel_id=1, source_target_pairs={{0,24},{8,16},{16,8},{24,0},{1,25},{9,17},{17,9},{25,1},{2,26},{10... | collective-permute-start | bytes 405512 | tf_op jit(solution)/shard_map/ppermute | solution.py:437
  35.6 6.8 %collective-permute-start.7 = (bf16[264,256]{1,0:T(8,128)(2,1)S(1)}, bf16[264,256]{1,0:T(8,128)(2,1)S(1)}, u32[]{:S(2)}, u32[]{:S(2)}) collective-permute-start(bf16[264,256]{1,0:T(8,128)(2,1)S(1)} %get-tuple-element.41), channel_id=1, source_target_pairs={{0,6},{1,7},{2,4},{3,5},{4,2},{5,3},{6,0},{7,1},{8,14},{9,15},{10,... | collective-permute-start | bytes 405512 | tf_op jit(solution)/shard_map/ppermute | solution.py:440
  38.4 5.7 %collective-permute-start.8 = (bf16[264,256]{1,0:T(8,128)(2,1)S(1)}, bf16[264,256]{1,0:T(8,128)(2,1)S(1)}, u32[]{:S(2)}, u32[]{:S(2)}) collective-permute-start(bf16[264,256]{1,0:T(8,128)(2,1)S(1)} %get-tuple-element.42), channel_id=1, source_target_pairs={{0,4},{1,5},{2,6},{3,7},{4,0},{5,1},{6,2},{7,3},{8,12},{9,13},{10,... | collective-permute-start | bytes 405512 | tf_op jit(solution)/shard_map/ppermute | solution.py:440
  38.9 5.3 %collective-permute-start.9 = (bf16[264,256]{1,0:T(8,128)(2,1)S(1)}, bf16[264,256]{1,0:T(8,128)(2,1)S(1)}, u32[]{:S(2)}, u32[]{:S(2)}) collective-permute-start(bf16[264,256]{1,0:T(8,128)(2,1)S(1)} %get-tuple-element.43), channel_id=1, source_target_pairs={{0,2},{1,3},{2,0},{3,1},{4,6},{5,7},{6,4},{7,5},{8,10},{9,11},{10,... | collective-permute-start | bytes 405512 | tf_op jit(solution)/shard_map/ppermute | solution.py:440
